TPU v7x, 32 devices: a whole 2x2x4 slice. The times are simulated.
32 devices in a mesh: dp: 32 (over z, y, x, core).
Axes of the slice: x: 2, y: 2, z: 4, core: 2. Of those that a mesh axis runs over, the one named last changes fastest.
Arguments:
- image_features: bfloat16 [4096, 1152], P('dp'), may hold values from -0.59765625 to 0.59765625
- text_features: bfloat16 [4096, 1152], P('dp'), may hold values from -0.59765625 to 0.59765625
- projections: bfloat16 [2304, 1152], P('dp'), may hold values from -0.1875 to 0.1875
- labels: int32 [4096], P('dp'), may hold values from 0 to 4095, as said below
Outputs:
- image_grad: float32 [4096, 1152], P('dp')
- text_grad: float32 [4096, 1152], P('dp')
Inputs may be any that keep to these rules, and one draw needn't show every extreme that they name: For each block k of 128 rows, the labels are the 128 text rows of one block (k - s) mod 32, each once, with s between 0 and 15 drawn for each block.
All inputs are finite; a program needn't handle non-finite values.
Results may differ from a plain program's by a relative error of at most 0.01.
Values may be sent and summed in bfloat16 or wider, within the bound.
A program may use at most 128 MiB of HBM per device.

v0:
```python
import jax
import jax.numpy as jnp
from jax import lax
from jax.sharding import PartitionSpec as P

REACH = 32


logit_scale = 10.0
logit_bias = -2.0
eps = 1e-06
contract_last = (((1,), (1,)), ((), ()))
contract_first = (((0,), (0,)), ((), ()))


def from_behind(value, axis, steps):
    count = lax.axis_size(axis)
    pairs = [(source, (source + steps) % count) for source in range(count)]
    return lax.ppermute(value, axis, pairs)


def normalize(raw):
    norm = jnp.sqrt(jnp.sum(raw * raw, axis=-1, keepdims=True) + eps)
    return (raw / norm, norm)


def unproject(unit, norm, grad):
    inner = jnp.sum(unit * grad, axis=-1, keepdims=True)
    return ((grad - unit * inner) / norm).astype(jnp.bfloat16)


def coefficients(left, right, left_labels, right_ids):
    logits = (
        logit_scale
        * lax.dot_general(left, right, contract_last, preferred_element_type=jnp.float32)
        + logit_bias
    )
    positive = (left_labels[:, None] == right_ids[None, :]).astype(jnp.float32)
    return (jax.nn.sigmoid(logits) - positive).astype(jnp.bfloat16)


def far_text(stack, span):
    return from_behind(stack, "dp", span)


def far_partial(stack, span):
    return from_behind(stack.astype(jnp.bfloat16), "dp", -span).astype(stack.dtype)


def per_device(image_features, text_features, projections, labels):
    rows, width_in = image_features.shape
    count = lax.axis_size("dp")
    index = lax.axis_index("dp")
    shifts = min(REACH, count // 2)
    whole = lax.all_gather(projections, "dp", axis=0, tiled=True)
    image_weight = whole[:width_in]
    text_weight = whole[width_in:]
    image_unit, image_norm = normalize(
        jnp.dot(image_features, image_weight, preferred_element_type=jnp.float32)
    )
    text_unit, text_norm = normalize(
        jnp.dot(text_features, text_weight, preferred_element_type=jnp.float32)
    )
    image_emb = image_unit.astype(jnp.bfloat16)
    text_emb = text_unit.astype(jnp.bfloat16)
    width = image_emb.shape[1]
    positions = jnp.arange(rows, dtype=jnp.int32)
    text_stack = text_emb[None]
    span = 1
    while span < shifts:
        taken = min(span, shifts - span)
        text_stack = jnp.concatenate([text_stack, far_text(text_stack, span)], axis=0)
        span = span * 2
    offsets = jnp.arange(shifts, dtype=jnp.int32)
    text_ids = (((index - offsets) % count)[:, None] * rows + positions[None, :]).reshape(-1)
    text_rows = text_stack.reshape(shifts * rows, width)
    coeff = coefficients(image_emb, text_rows, labels, text_ids)
    image_acc = logit_scale * jnp.dot(coeff, text_rows, preferred_element_type=jnp.float32)
    partials = logit_scale * lax.dot_general(
        coeff, image_emb, contract_first, preferred_element_type=jnp.float32
    )
    partials = partials.reshape(shifts, rows, width)
    length = shifts
    while length > 1:
        half = (length + 1) // 2
        moved = far_partial(partials[half:length], half)
        partials = partials[:half].at[: length - half].add(moved)
        length = half
    text_acc = partials[0]
    image_draw = unproject(image_unit, image_norm, image_acc)
    text_draw = unproject(text_unit, text_norm, text_acc)
    image_grad = lax.dot_general(
        image_draw, image_weight, contract_last, preferred_element_type=jnp.float32
    )
    text_grad = lax.dot_general(
        text_draw, text_weight, contract_last, preferred_element_type=jnp.float32
    )
    return (image_grad, text_grad)


def solution(mesh):
    placed = (P("dp", None), P("dp", None), P("dp", None), P("dp"))
    return jax.shard_map(
        per_device,
        mesh=mesh,
        in_specs=placed,
        out_specs=(P("dp", None), P("dp", None)),
        check_vma=False,
    )
```

profile of v0, /device:TPU:0, one launch (start us, length us, event | category | flops | bytes accessed | tf_op | source)
XLA Modules:
  0.0 301.1 jit_solution(4069287338948198136)
XLA Ops:
  7.2 0.0 copy-start
  7.2 0.0 all-gather.2.cloned.1.call-start
  7.2 0.7 all-gather.2.cloned.1.call-update
  7.9 71.3 %all-gather.2.cloned.1.call-done = bf16[2304,1152]{1,0:T(8,128)(2,1)} async-done(((bf16[72,1152]{1,0:T(8,128)(2,1)}), bf16[2304,1152]{1,0:T(8,128)(2,1)}) %all-gather.2.cloned.1.call-update) | async-done | bytes 5308432 | tf_op jit(solution)/shard_map/all_gather | solution.py:55
  79.2 0.0 copy-done
  79.3 2.4 multiply_reduce_fusion.2
  81.7 0.9 constant_dynamic-update-slice_fusion.4
  82.6 0.3 collective-permute-start
  82.8 9.5 %collective-permute-done = bf16[1,128,1152]{2,1,0:T(8,128)(2,1)S(1)} collective-permute-done((bf16[1,128,1152]{2,1,0:T(8,128)(2,1)S(1)}, bf16[1,128,1152]{2,1,0:T(8,128)(2,1)S(1)}, u32[]{:S(2)}, u32[]{:S(2)}) %collective-permute-start) | collective-permute-done | bytes 294944 | tf_op jit(solution)/shard_map/ppermute | solution.py:19
  92.3 0.1 pad_maximum_fusion.2
  92.4 0.1 collective-permute-start.1
  92.5 14.3 %collective-permute-done.1 = bf16[2,128,1152]{2,1,0:T(8,128)(2,1)S(1)} collective-permute-done((bf16[2,128,1152]{2,1,0:T(8,128)(2,1)S(1)}, bf16[2,128,1152]{2,1,0:T(8,128)(2,1)S(1)}, u32[]{:S(2)}, u32[]{:S(2)}) %collective-permute-start.1) | collective-permute-done | bytes 589856 | tf_op jit(solution)/shard_map/ppermute | solution.py:19
  106.7 0.1 pad_maximum_fusion.1
  106.9 0.0 copy-start.1
  106.9 0.1 collective-permute-start.2
  107.0 25.2 %collective-permute-done.2 = bf16[4,128,1152]{2,1,0:T(8,128)(2,1)S(1)} collective-permute-done((bf16[4,128,1152]{2,1,0:T(8,128)(2,1)S(1)}, bf16[4,128,1152]{2,1,0:T(8,128)(2,1)S(1)}, u32[]{:S(2)}, u32[]{:S(2)}) %collective-permute-start.2) | collective-permute-done | bytes 1179680 | tf_op jit(solution)/shard_map/ppermute | solution.py:19
  132.1 1.7 pad_maximum_fusion
  133.9 0.1 collective-permute-start.3
  134.0 0.1 add_bitcast_fusion
  134.1 2.4 multiply_reduce_fusion.3
  136.5 0.7 constant_dynamic-update-slice_fusion.3
  137.3 0.9 constant_dynamic-update-slice_fusion.2
  138.2 1.1 constant_dynamic-update-slice_fusion.1
  139.3 43.6 %collective-permute-done.3 = bf16[8,128,1152]{2,1,0:T(8,128)(2,1)} collective-permute-done((bf16[8,128,1152]{2,1,0:T(8,128)(2,1)}, bf16[8,128,1152]{2,1,0:T(8,128)(2,1)}, u32[]{:S(2)}, u32[]{:S(2)}) %collective-permute-start.3) | collective-permute-done | bytes 2359328 | tf_op jit(solution)/shard_map/ppermute | solution.py:19
  182.9 3.3 %constant_dynamic-update-slice_fusion = bf16[16,128,1152]{2,1,0:T(8,128)(2,1)} fusion(bf16[16,128,1152]{2,1,0:T(8,128)(2,1)} %constant_dynamic-update-slice_fusion.1, bf16[8,128,1152]{2,1,0:T(8,128)(2,1)} %collective-permute-done.3), kind=kLoop, calls=%fused_computation.45 | loop fusion | bytes 4718592 | tf_op jit(solution)/shard_map/concatenate | solution.py:72
  186.2 4.1 %fusion.6 = bf16[128,2048]{1,0:T(8,128)(2,1)S(1)} fusion(bf16[2048,1152]{1,0:T(8,128)(2,1)} %bitcast.23, s32[2048]{0:T(1024)S(1)} %add_bitcast_fusion, s32[128]{0:T(128)S(1)} %copy-done.2, f32[128,1152]{1,0:T(8,128)S(1)} %get-tuple-element.87, f32[128]{0:T(128)S(1)} %add_sqrt_fusion.1), kind=kOutput, calls=%fused_computation.11 | convolution fusion | flops 606633984 | bytes 5841920 | tf_op jit(solution)/shard_map/dot_general | solution.py:35
  190.3 1.5 convolution_multiply_fusion
  191.8 0.2 slice.157
  192.0 0.9 collective-permute-start.4
  192.9 0.3 slice.127
  193.2 45.9 %collective-permute-done.4 = bf16[8,128,1152]{2,1,0:T(8,128)(2,1)S(1)} collective-permute-done((bf16[8,128,1152]{2,1,0:T(8,128)(2,1)S(1)}, bf16[8,128,1152]{2,1,0:T(8,128)(2,1)S(1)}, u32[]{:S(2)}, u32[]{:S(2)}) %collective-permute-start.4) | collective-permute-done | bytes 2359328 | tf_op jit(solution)/shard_map/ppermute | solution.py:19
  239.1 0.4 convert_add_fusion
  239.5 0.1 slice.158
  239.7 7.5 %collective-permute-start.5 = (bf16[4,128,1152]{2,1,0:T(8,128)(2,1)S(1)}, bf16[4,128,1152]{2,1,0:T(8,128)(2,1)S(1)}, u32[]{:S(2)}, u32[]{:S(2)}) collective-permute-start(bf16[4,128,1152]{2,1,0:T(8,128)(2,1)S(1)} %slice.158), channel_id=1, source_target_pairs={{0,28},{1,29},{2,30},{3,31},{4,0},{5,1},{6,2},{7,3},{8,4},{9,5},{1... | collective-permute-start | bytes 3538952 | tf_op jit(solution)/shard_map/ppermute | solution.py:19
  247.2 21.3 %collective-permute-done.5 = bf16[4,128,1152]{2,1,0:T(8,128)(2,1)S(1)} collective-permute-done((bf16[4,128,1152]{2,1,0:T(8,128)(2,1)S(1)}, bf16[4,128,1152]{2,1,0:T(8,128)(2,1)S(1)}, u32[]{:S(2)}, u32[]{:S(2)}) %collective-permute-start.5) | collective-permute-done | bytes 1179680 | tf_op jit(solution)/shard_map/ppermute | solution.py:19
  268.5 0.3 slice_add_fusion
  268.8 0.0 slice-start.2
  268.8 0.1 slice.159
  268.9 0.0 slice-start.3
  268.9 9.6 %collective-permute-start.6 = (bf16[2,128,1152]{2,1,0:T(8,128)(2,1)S(1)}, bf16[2,128,1152]{2,1,0:T(8,128)(2,1)S(1)}, u32[]{:S(2)}, u32[]{:S(2)}) collective-permute-start(bf16[2,128,1152]{2,1,0:T(8,128)(2,1)S(1)} %slice.159), channel_id=1, source_target_pairs={{0,30},{1,31},{2,0},{3,1},{4,2},{5,3},{6,4},{7,5},{8,6},{9,7},{10,... | collective-permute-start | bytes 1769480 | tf_op jit(solution)/shard_map/ppermute | solution.py:19
  278.4 1.0 multiply_reduce_fusion.1
  279.4 7.7 %collective-permute-done.6 = bf16[2,128,1152]{2,1,0:T(8,128)(2,1)S(1)} collective-permute-done((bf16[2,128,1152]{2,1,0:T(8,128)(2,1)S(1)}, bf16[2,128,1152]{2,1,0:T(8,128)(2,1)S(1)}, u32[]{:S(2)}, u32[]{:S(2)}) %collective-permute-start.6) | collective-permute-done | bytes 589856 | tf_op jit(solution)/shard_map/ppermute | solution.py:19
  287.1 0.1 slice_add_fusion.1
  287.2 0.8 collective-permute-start.7
  288.0 1.8 fusion.11
  289.8 2.5 collective-permute-done.7
  292.3 0.2 multiply_reduce_fusion
  292.5 1.8 fusion.7
  (15 shorter events, 0.1 us)
Async XLA Ops:
  7.2 72.1 %copy-start = (bf16[128,1152]{1,0:T(8,128)(2,1)S(1)}, bf16[128,1152]{1,0:T(8,128)(2,1)}, u32[]{:S(2)}) copy-start(bf16[128,1152]{1,0:T(8,128)(2,1)} %param.21) | copy-start | bytes 884740
  7.2 72.1 %all-gather.2.cloned.1.call-start = ((), (), s32[]{:S(2)}) async-start(), calls=%async_computation | async-start | bytes 5474304 | tf_op jit(solution)/shard_map/all_gather | solution.py:55
  82.6 9.7 %collective-permute-start = (bf16[1,128,1152]{2,1,0:T(8,128)(2,1)S(1)}, bf16[1,128,1152]{2,1,0:T(8,128)(2,1)S(1)}, u32[]{:S(2)}, u32[]{:S(2)}) collective-permute-start(bf16[1,128,1152]{2,1,0:T(8,128)(2,1)S(1)} %get-tuple-element.83), channel_id=1, source_target_pairs={{0,1},{1,2},{2,3},{3,4},{4,5},{5,6},{6,7},{7,8},{8,9},{9,10},{10,1... | collective-permute-start | bytes 884744 | tf_op jit(solution)/shard_map/ppermute | solution.py:19
  92.4 14.4 %collective-permute-start.1 = (bf16[2,128,1152]{2,1,0:T(8,128)(2,1)S(1)}, bf16[2,128,1152]{2,1,0:T(8,128)(2,1)S(1)}, u32[]{:S(2)}, u32[]{:S(2)}) collective-permute-start(bf16[2,128,1152]{2,1,0:T(8,128)(2,1)S(1)} %pad_maximum_fusion.2), channel_id=1, source_target_pairs={{0,2},{1,3},{2,4},{3,5},{4,6},{5,7},{6,8},{7,9},{8,10},{9,11},{10,... | collective-permute-start | bytes 1769480 | tf_op jit(solution)/shard_map/ppermute | solution.py:19
  106.9 27.2 %copy-start.1 = (bf16[128,1152]{1,0:T(8,128)(2,1)S(1)}, bf16[128,1152]{1,0:T(8,128)(2,1)}, u32[]{:S(2)}) copy-start(bf16[128,1152]{1,0:T(8,128)(2,1)} %param.20) | copy-start | bytes 884740
  106.9 25.2 %collective-permute-start.2 = (bf16[4,128,1152]{2,1,0:T(8,128)(2,1)S(1)}, bf16[4,128,1152]{2,1,0:T(8,128)(2,1)S(1)}, u32[]{:S(2)}, u32[]{:S(2)}) collective-permute-start(bf16[4,128,1152]{2,1,0:T(8,128)(2,1)S(1)} %pad_maximum_fusion.1), channel_id=1, source_target_pairs={{0,4},{1,5},{2,6},{3,7},{4,8},{5,9},{6,10},{7,11},{8,12},{9,13},{1... | collective-permute-start | bytes 3538952 | tf_op jit(solution)/shard_map/ppermute | solution.py:19
  133.9 49.0 %collective-permute-start.3 = (bf16[8,128,1152]{2,1,0:T(8,128)(2,1)}, bf16[8,128,1152]{2,1,0:T(8,128)(2,1)}, u32[]{:S(2)}, u32[]{:S(2)}) collective-permute-start(bf16[8,128,1152]{2,1,0:T(8,128)(2,1)} %pad_maximum_fusion), channel_id=1, source_target_pairs={{0,8},{1,9},{2,10},{3,11},{4,12},{5,13},{6,14},{7,15},{8,16},{9,17... | collective-permute-start | bytes 7077896 | tf_op jit(solution)/shard_map/ppermute | solution.py:19
  139.3 47.0 %copy-start.2 = (s32[128]{0:T(128)S(1)}, s32[128]{0:T(128)}, u32[]{:S(2)}) copy-start(s32[128]{0:T(128)} %param.23) | copy-start | bytes 1540
  192.0 47.1 %collective-permute-start.4 = (bf16[8,128,1152]{2,1,0:T(8,128)(2,1)S(1)}, bf16[8,128,1152]{2,1,0:T(8,128)(2,1)S(1)}, u32[]{:S(2)}, u32[]{:S(2)}) collective-permute-start(bf16[8,128,1152]{2,1,0:T(8,128)(2,1)S(1)} %bitcast.22), channel_id=1, source_target_pairs={{0,24},{1,25},{2,26},{3,27},{4,28},{5,29},{6,30},{7,31},{8,0},{9,1... | collective-permute-start | bytes 7077896 | tf_op jit(solution)/shard_map/ppermute | solution.py:19
  192.9 85.5 %slice-start = ((s8[4718592]{0:T(1024)(128)(4,1)}), s8[4194304]{0:T(1024)(128)(4,1)S(1)}, s32[]{:S(2)}) async-start(s8[4718592]{0:T(1024)(128)(4,1)} %bitcast.24), calls=%async_computation.1 | async-start | bytes 8388608
  239.1 39.3 %slice-start.1 = ((s8[4718592]{0:T(1024)(128)(4,1)}), s8[524288]{0:T(1024)(128)(4,1)S(1)}, s32[]{:S(2)}) async-start(s8[4718592]{0:T(1024)(128)(4,1)} %bitcast.24), calls=%async_computation.2 | async-start | bytes 1048576
  239.7 28.9 %collective-permute-start.5 = (bf16[4,128,1152]{2,1,0:T(8,128)(2,1)S(1)}, bf16[4,128,1152]{2,1,0:T(8,128)(2,1)S(1)}, u32[]{:S(2)}, u32[]{:S(2)}) collective-permute-start(bf16[4,128,1152]{2,1,0:T(8,128)(2,1)S(1)} %slice.158), channel_id=1, source_target_pairs={{0,28},{1,29},{2,30},{3,31},{4,0},{5,1},{6,2},{7,3},{8,4},{9,5},{1... | collective-permute-start | bytes 3538952 | tf_op jit(solution)/shard_map/ppermute | solution.py:19
  268.8 19.2 %slice-start.2 = ((s8[5308416]{0:T(1024)(128)(4,1)}), s8[4194304]{0:T(1024)(128)(4,1)S(1)}, s32[]{:S(2)}) async-start(s8[5308416]{0:T(1024)(128)(4,1)} %bitcast.27), calls=%async_computation.3 | async-start | bytes 8388608
  268.9 19.1 %slice-start.3 = ((s8[5308416]{0:T(1024)(128)(4,1)}), s8[1114112]{0:T(1024)(128)(4,1)S(1)}, s32[]{:S(2)}) async-start(s8[5308416]{0:T(1024)(128)(4,1)} %bitcast.27), calls=%async_computation.4 | async-start | bytes 2228224
  268.9 18.2 %collective-permute-start.6 = (bf16[2,128,1152]{2,1,0:T(8,128)(2,1)S(1)}, bf16[2,128,1152]{2,1,0:T(8,128)(2,1)S(1)}, u32[]{:S(2)}, u32[]{:S(2)}) collective-permute-start(bf16[2,128,1152]{2,1,0:T(8,128)(2,1)S(1)} %slice.159), channel_id=1, source_target_pairs={{0,30},{1,31},{2,0},{3,1},{4,2},{5,3},{6,4},{7,5},{8,6},{9,7},{10,... | collective-permute-start | bytes 1769480 | tf_op jit(solution)/shard_map/ppermute | solution.py:19
  287.2 5.0 %collective-permute-start.7 = (bf16[1,128,1152]{2,1,0:T(8,128)(2,1)S(1)}, bf16[1,128,1152]{2,1,0:T(8,128)(2,1)S(1)}, u32[]{:S(2)}, u32[]{:S(2)}) collective-permute-start(bf16[1,128,1152]{2,1,0:T(8,128)(2,1)S(1)} %slice.160), channel_id=1, source_target_pairs={{0,31},{1,0},{2,1},{3,2},{4,3},{5,4},{6,5},{7,6},{8,7},{9,8},{10,9... | collective-permute-start | bytes 884744 | tf_op jit(solution)/shard_map/ppermute | solution.py:19
Sparse Core Ops, SparseCore 0:
  10.9 68.2 all-gather.1
where the time goes:
time: 302 us; the launch traced here: 301 us
  waiting for transfers between devices  242 us (80%)
  starting transfers between devices  19.3 us (6%)
  matrix products  14.9 us (5%)
  between operations  14.2 us (5%)
  local copies, waits for them, and re-layouts  6.85 us (2%)
  other arithmetic  3.88 us (1%)
    ppermute x8, waiting for transfers between devices, from_behind(): return lax.ppermute(value, axis, pairs)  170 us
    all_gather x1, waiting for transfers between devices, per_device(): whole = lax.all_gather(projections, 'dp', axis=0, tiled=True)  71.3 us
    ppermute x8, starting transfers between devices, from_behind(): return lax.ppermute(value, axis, pairs)  19.2 us
  transfers between devices with their start and end apart: 9, of which 9 were waited for; matrix products, arithmetic and copies ran while one was open for 3% of the time, Pallas kernels for 0%

commit v1 on v0

v1 whole, which is shorter than its diff:
```python
import functools

import jax
import jax.numpy as jnp
from jax import lax
from jax.experimental import pallas as pl
from jax.experimental.pallas import tpu as pltpu
from jax.sharding import PartitionSpec as P

REACH = 32


logit_scale = 10.0
logit_bias = -2.0
eps = 1e-06
contract_last = (((1,), (1,)), ((), ()))
MESH = pl.DeviceIdType.MESH


def normalize(raw):
    norm = jnp.sqrt(jnp.sum(raw * raw, axis=-1, keepdims=True) + eps)
    return (raw / norm, norm)


def unproject(unit, norm, grad):
    inner = jnp.sum(unit * grad, axis=-1, keepdims=True)
    return ((grad - unit * inner) / norm).astype(jnp.bfloat16)


def pair_kernel(
    count, shifts,
    image_ref, text_ref, label_ref, image_acc, text_acc,
    images, texts, names, coeff, coeff_t, over, over_in, total, total_in, back, back_in,
    send, recv,
):
    rows, width = image_ref.shape
    group = shifts // 2
    chips = group // 2
    planes = count // group
    me = lax.axis_index("dp")
    plane, inside = me // group, me % group
    chip, core = inside // 2, inside % 2
    partner = me + 1 - 2 * core

    def chip_at(step):
        return plane * group + lax.rem(chip + step + chips, chips) * 2 + core

    def plane_at(step):
        return lax.rem(plane + step + planes, planes) * group + inside

    barrier = pltpu.get_barrier_semaphore()
    others = [chip_at(step) for step in range(1, chips)]
    others += [plane_at(step) for step in (1, 2, -1, -2)] + [partner]
    for other in others:
        pl.semaphore_signal(barrier, inc=1, device_id=(other,), device_id_type=MESH)
    pl.semaphore_wait(barrier, len(others))

    made = []

    def copy(src, dst, to):
        at = len(made)
        made.append(
            pltpu.make_async_remote_copy(
                src_ref=src, dst_ref=dst, send_sem=send.at[at], recv_sem=recv.at[at],
                device_id=(to,), device_id_type=MESH,
            )
        )
        return made[-1]

    near, far = pl.ds(0, rows), pl.ds(rows, rows)
    text_copies = [copy(text_ref, texts.at[step], plane_at(step)) for step in (1, 2)]
    image_copies, name_copies = [None], [None]
    for step in range(1, chips):
        to = chip_at(step)
        name_copies.append(copy(label_ref, names.at[step, 0], to))
        image_copies.append(copy(image_ref, images.at[step, near], to))
    for one in text_copies + image_copies[1:] + name_copies[1:]:
        one.start()
    across = [
        copy(label_ref, names.at[0, 1], partner),
        copy(image_ref, images.at[0, far], partner),
    ]
    for one in across:
        one.start()
    images[0, near] = image_ref[...]
    names[0, 0] = label_ref[...]
    texts[0] = text_ref[...]
    for step in range(1, chips):
        name_copies[step].wait_recv()
        image_copies[step].wait_recv()
        passed = [
            copy(names.at[step, 0], names.at[step, 1], partner),
            copy(images.at[step, near], images.at[step, far], partner),
        ]
        for one in passed:
            one.start()
        across += passed
    for one in across:
        one.wait_recv()

    lane = lax.broadcasted_iota(jnp.int32, (rows, 1), 0)
    back_copies = []
    for age in range(3):
        if age > 0:
            text_copies[age - 1].wait_recv()
        text_block = lax.rem(me - age * group + count, count)
        ids = text_block * rows + lane
        text = texts[age]

        def fill(step, carry):
            source = lax.rem(chip - step + chips, chips)
            logits = logit_scale * lax.dot_general(
                text, images[step], contract_last, preferred_element_type=jnp.float32
            ) + logit_bias
            for side in range(2):
                block = plane * group + source * 2 + (core if side == 0 else 1 - core)
                shift = lax.rem(block - text_block + count, count)
                piece = jax.nn.sigmoid(logits[:, side * rows : (side + 1) * rows])
                piece = piece - (names[step, side] == ids).astype(jnp.float32)
                piece = piece * (shift < shifts).astype(jnp.float32)
                coeff[step, age, :, side * rows : (side + 1) * rows] = piece.astype(jnp.bfloat16)
                coeff_t[step, side * rows : (side + 1) * rows, age * rows : (age + 1) * rows] = (
                    piece.T.astype(jnp.bfloat16)
                )
            return carry

        lax.fori_loop(0, chips, fill, 0)

        def add(step, carry):
            text_acc[...] += jnp.dot(
                coeff[step, age], images[step], preferred_element_type=jnp.float32
            )
            return carry

        text_acc[...] = jnp.zeros_like(text_acc)
        lax.fori_loop(0, chips, add, 0)
        if age == 0:
            image_acc[...] = text_acc[...]
        else:
            back[age - 1] = (logit_scale * text_acc[...]).astype(jnp.bfloat16)
            back_copies.append(copy(back.at[age - 1], back_in.at[age - 1], plane_at(-age)))
            back_copies[-1].start()
    text_acc[...] = logit_scale * image_acc[...]

    rest = texts[...].reshape(3 * rows, width)

    def image_part(step, side):
        return logit_scale * jnp.dot(
            coeff_t[step, side * rows : (side + 1) * rows], rest,
            preferred_element_type=jnp.float32,
        )

    over_copies = []
    steps = list(range(1, chips)) + [0]
    for step in steps:
        over[step] = image_part(step, 1).astype(jnp.bfloat16)
        over_copies.append(copy(over.at[step], over_in.at[step], partner))
        over_copies[-1].start()
    total_copies = []
    for at, step in enumerate(steps):
        mine = image_part(step, 0)
        over_copies[at].wait_recv()
        mine = mine + over_in[step].astype(jnp.float32)
        if step == 0:
            image_acc[...] = mine
        else:
            total[step] = mine.astype(jnp.bfloat16)
            total_copies.append(copy(total.at[step], total_in.at[step], chip_at(-step)))
            total_copies[-1].start()
    for at in range(chips - 1):
        total_copies[at].wait_recv()
        image_acc[...] += total_in[at + 1].astype(jnp.float32)
    for age in range(2):
        back_copies[age].wait_recv()
        text_acc[...] += back_in[age].astype(jnp.float32)
    for one in made:
        one.wait_send()


def pair_grads(image_emb, text_emb, labels, count, shifts):
    rows, width = image_emb.shape
    chips = shifts // 4
    low = jnp.bfloat16
    copies = 2 + 6 * chips + 2
    vmem = pl.BlockSpec(memory_space=pltpu.VMEM)
    return pl.pallas_call(
        functools.partial(pair_kernel, count, shifts),
        out_shape=[jax.ShapeDtypeStruct((rows, width), jnp.float32)] * 2,
        in_specs=[vmem] * 3,
        out_specs=[vmem] * 2,
        scratch_shapes=[
            pltpu.VMEM((chips, 2 * rows, width), low),
            pltpu.VMEM((3, rows, width), low),
            pltpu.VMEM((chips, 2, 1, rows), jnp.int32),
            pltpu.VMEM((chips, 3, rows, 2 * rows), low),
            pltpu.VMEM((chips, 2 * rows, 3 * rows), low),
            pltpu.VMEM((chips, rows, width), low),
            pltpu.VMEM((chips, rows, width), low),
            pltpu.VMEM((chips, rows, width), low),
            pltpu.VMEM((chips, rows, width), low),
            pltpu.VMEM((2, rows, width), low),
            pltpu.VMEM((2, rows, width), low),
            pltpu.SemaphoreType.DMA((copies,)),
            pltpu.SemaphoreType.DMA((copies,)),
        ],
        compiler_params=pltpu.CompilerParams(
            collective_id=0, has_side_effects=True, vmem_limit_bytes=60 * 1024 * 1024
        ),
    )(image_emb, text_emb, labels.reshape(1, rows))


def per_device(image_features, text_features, projections, labels):
    rows, width_in = image_features.shape
    count = lax.axis_size("dp")
    shifts = min(REACH, count // 2)
    whole = lax.all_gather(projections, "dp", axis=0, tiled=True)
    image_weight = whole[:width_in]
    text_weight = whole[width_in:]
    image_unit, image_norm = normalize(
        jnp.dot(image_features, image_weight, preferred_element_type=jnp.float32)
    )
    text_unit, text_norm = normalize(
        jnp.dot(text_features, text_weight, preferred_element_type=jnp.float32)
    )
    image_acc, text_acc = pair_grads(
        image_unit.astype(jnp.bfloat16), text_unit.astype(jnp.bfloat16), labels, count, shifts
    )
    image_draw = unproject(image_unit, image_norm, image_acc)
    text_draw = unproject(text_unit, text_norm, text_acc)
    image_grad = lax.dot_general(
        image_draw, image_weight, contract_last, preferred_element_type=jnp.float32
    )
    text_grad = lax.dot_general(
        text_draw, text_weight, contract_last, preferred_element_type=jnp.float32
    )
    return (image_grad, text_grad)


def solution(mesh):
    placed = (P("dp", None), P("dp", None), P("dp", None), P("dp"))
    return jax.shard_map(
        per_device,
        mesh=mesh,
        in_specs=placed,
        out_specs=(P("dp", None), P("dp", None)),
        check_vma=False,
    )
```

time: 302 us -> 148 us (0.49)
  waiting for transfers between devices: 242 us -> 72 us
  Pallas kernels: 0 us -> 48.2 us
  starting transfers between devices: 19.3 us -> 0.04 us
  local copies, waits for them, and re-layouts: 6.85 us -> 0.02 us
  matrix products: 14.9 us -> 10.6 us
    ppermute x8 -> x0, waiting for transfers between devices: 170 us -> none  [from_behind(): return lax.ppermute(value, axis, pairs)]
    pallas_call x0 -> x1, Pallas kernels: none -> 48.2 us  [pair_grads(): pl.pallas_call(functools.partial(pair_kernel, count, shifts), out_shape=[...]
    ppermute x8 -> x0, starting transfers between devices: 19.2 us -> none  [from_behind(): return lax.ppermute(value, axis, pairs)]
    dot_general x3 -> x0, matrix products: 6.5 us -> none  [the longest x1 4.05 us: coefficients(): lax.dot_general(left, right, contract_last, preferred_element_type=jnp.fl...]
    concatenate x1 -> x0, local copies, waits for them, and re-layouts: 3.33 us -> none  [per_device(): jnp.concatenate([text_stack, far_text(text_stack, span)], axis=0)]
  transfers between devices with their start and end apart: 9 -> 1, of which waited for: 9 -> 1; matrix products, arithmetic and copies ran while one was open for 3% -> 0% of each run, Pallas kernels for 0% -> 0%
where the time goes in v1:
time: 148 us
  waiting for transfers between devices  72 us (49%)
  Pallas kernels  48.2 us (33%)
  between operations  14.1 us (10%)
  matrix products  10.6 us (7%)
  other arithmetic  3.36 us (2%)
    all_gather x1, waiting for transfers between devices, per_device(): whole = lax.all_gather(projections, 'dp', axis=0, tiled=True)  71.3 us
    pallas_call x1, Pallas kernels, pair_grads(): pl.pallas_call(functools.partial(pair_kernel, count, shifts), out_shape=[...  48.2 us
    dot_general x1, matrix products, per_device(): lax.dot_general(image_draw, image_weight, contract_last, preferred_elemen...  3.8 us
  transfers between devices with their start and end apart: 1, of which 1 were waited for; matrix products, arithmetic and copies ran while one was open for 0% of the time, Pallas kernels for 0%

profile of v1, /device:TPU:0, one launch (start us, length us, event | category | flops | bytes accessed | tf_op | source)
XLA Modules:
  0.0 148.3 jit_solution(16205212164642280666)
XLA Ops:
  7.2 0.0 copy-start
  7.2 0.0 all-gather.2.cloned.1.call-start
  7.2 0.7 all-gather.2.cloned.1.call-update
  7.9 71.3 %all-gather.2.cloned.1.call-done = bf16[2304,1152]{1,0:T(8,128)(2,1)} async-done(((bf16[72,1152]{1,0:T(8,128)(2,1)}), bf16[2304,1152]{1,0:T(8,128)(2,1)}) %all-gather.2.cloned.1.call-update) | async-done | bytes 5308432 | tf_op jit(solution)/shard_map/all_gather | solution.py:216
  79.2 0.0 copy-done
  79.3 2.4 %multiply_reduce_fusion.2 = (f32[128]{0:T(128)S(1)}, f32[128,1152]{1,0:T(8,128)S(1)}) fusion(bf16[128,1152]{1,0:T(8,128)(2,1)S(1)} %copy-done, bf16[2304,1152]{1,0:T(8,128)(2,1)} %all-gather.2.cloned.1.call-done), kind=kOutput, calls=%fused_computation.12 | convolution fusion | flops 340033408 | bytes 3539456 | tf_op jit(solution)/shard_map/dot_general | solution.py:223
  81.7 2.6 %multiply_reduce_fusion.3 = (f32[128]{0:T(128)S(1)}, f32[128,1152]{1,0:T(8,128)S(1)}) fusion(bf16[128,1152]{1,0:T(8,128)(2,1)} %param.4, bf16[2304,1152]{1,0:T(8,128)(2,1)} %all-gather.2.cloned.1.call-done), kind=kOutput, calls=%fused_computation.13 | convolution fusion | flops 340033408 | bytes 3539456 | tf_op jit(solution)/shard_map/dot_general | solution.py:220
  84.3 0.8 fusion.13.text_ref
  85.1 0.8 fusion.12.image_ref
  85.9 48.2 %shard_map.59 = (f32[128,1152]{1,0:T(8,128)}, f32[128,1152]{1,0:T(8,128)}) custom-call(bf16[128,1152]{1,0:T(8,128)(2,1)} %fusion.12.image_ref, bf16[128,1152]{1,0:T(8,128)(2,1)} %fusion.13.text_ref, s32[1,128]{1,0:T(1,128)} %bitcast.3), custom_call_target="tpu_custom_call" | custom-call | tf_op jit(solution)/shard_map/pallas_call | solution.py:186
  134.1 0.0 copy-start.1
  134.1 0.0 slice-start
  134.1 1.7 %multiply_reduce_fusion = (f32[128]{0:T(128)S(1)}, f32[128]{0:T(128)S(1)}) fusion(f32[128,1152]{1,0:T(8,128)} %get-tuple-element.5, f32[128,1152]{1,0:T(8,128)S(1)} %get-tuple-element.9, f32[128]{0:T(128)S(1)} %add_sqrt_fusion, f32[128,1152]{1,0:T(8,128)} %get-tuple-element.4, f32[128,1152]{1,0:T(8,128)S(1)} %get-tuple-element.7, f32[128]{0:T(128)S(1)} %add_sqrt_fusion.1), kind=kLoop, calls=%fused_computation.9 | loop fusion | flops 884480 | bytes 2361344 | tf_op jit(solution)/shard_map/reduce_sum | solution.py:26
  135.8 0.0 slice-start.1
  135.8 3.8 %fusion.4 = f32[128,1152]{1,0:T(8,128)} fusion(bf16[2304,1152]{1,0:T(8,128)(2,1)} %all-gather.2.cloned.1.call-done, f32[128,1152]{1,0:T(8,128)} %get-tuple-element.4, f32[128]{0:T(128)S(1)} %get-tuple-element.11, f32[128]{0:T(128)S(1)} %add_sqrt_fusion.1, f32[128,1152]{1,0:T(8,128)S(1)} %get-tuple-element.7), kind=kOutput, calls=%fused_computation.4 | convolution fusion | flops 340475904 | bytes 4424704 | tf_op jit(solution)/shard_map/dot_general | solution.py:230
  139.6 0.0 copy-done.1
  139.6 0.0 slice-done
  139.6 0.0 slice-done.1
  139.7 1.8 %fusion = f32[128,1152]{1,0:T(8,128)} fusion(bf16[2304,1152]{1,0:T(8,128)(2,1)S(1)} %bitcast.5, f32[128,1152]{1,0:T(8,128)S(1)} %copy-done.1, f32[128]{0:T(128)S(1)} %get-tuple-element.10, f32[128]{0:T(128)S(1)} %add_sqrt_fusion, f32[128,1152]{1,0:T(8,128)S(1)} %get-tuple-element.9), kind=kOutput, calls=%fused_computation | convolution fusion | flops 340475904 | bytes 4424704 | tf_op jit(solution)/shard_map/dot_general | solution.py:233
  (3 shorter events, 0.0 us)
Async XLA Ops:
  7.2 72.1 %copy-start = (bf16[128,1152]{1,0:T(8,128)(2,1)S(1)}, bf16[128,1152]{1,0:T(8,128)(2,1)}, u32[]{:S(2)}) copy-start(bf16[128,1152]{1,0:T(8,128)(2,1)} %param.5) | copy-start | bytes 884740
  7.2 72.1 %all-gather.2.cloned.1.call-start = ((), (), s32[]{:S(2)}) async-start(), calls=%async_computation | async-start | bytes 5474304 | tf_op jit(solution)/shard_map/all_gather | solution.py:216
  134.1 5.5 %copy-start.1 = (f32[128,1152]{1,0:T(8,128)S(1)}, f32[128,1152]{1,0:T(8,128)}, u32[]{:S(2)}) copy-start(f32[128,1152]{1,0:T(8,128)} %get-tuple-element.5) | copy-start | bytes 1769476
  134.1 5.5 %slice-start = ((s8[5308416]{0:T(1024)(128)(4,1)}), s8[4194304]{0:T(1024)(128)(4,1)S(1)}, s32[]{:S(2)}) async-start(s8[5308416]{0:T(1024)(128)(4,1)} %bitcast.4), calls=%async_computation.1 | async-start | bytes 8388608
  135.8 3.8 %slice-start.1 = ((s8[5308416]{0:T(1024)(128)(4,1)}), s8[1114112]{0:T(1024)(128)(4,1)S(1)}, s32[]{:S(2)}) async-start(s8[5308416]{0:T(1024)(128)(4,1)} %bitcast.4), calls=%async_computation.2 | async-start | bytes 2228224
Sparse Core Ops, SparseCore 0:
  10.9 68.2 all-gather.1

commit v2 on v1

--- a/solution.py
+++ b/solution.py
@@ -209,11 +209,100 @@
     )(image_emb, text_emb, labels.reshape(1, rows))
 
 
+def gather_kernel(count, group, shard_ref, whole_ref, send, recv):
+    chips, planes = group // 2, count // group
+    me = lax.axis_index("dp")
+    plane, inside = me // group, me % group
+    chip, core = inside // 2, inside % 2
+    partner = me + 1 - 2 * core
+    relayed = chips == 4
+    if relayed:
+        low, high = chip + 1 - 2 * lax.rem(chip, 2), lax.rem(chip + 2, 4)
+        peers = [low + (high - low) * core, high + (low - high) * core]
+        sources = peers
+    else:
+        peers = [lax.rem(chip + step, chips) for step in range(1, chips)]
+        sources = [lax.rem(chip + chips - step, chips) for step in range(1, chips)]
+
+    def plane_at(step):
+        return lax.rem(plane + step + planes, planes)
+
+    def device(plane, chip):
+        return plane * group + chip * 2 + core
+
+    barrier = pltpu.get_barrier_semaphore()
+    others = [device(plane, peer) for peer in peers]
+    others += [device(plane_at(step), chip) for step in range(1, planes)] + [partner]
+    for other in others:
+        pl.semaphore_signal(barrier, inc=1, device_id=(other,), device_id_type=MESH)
+    pl.semaphore_wait(barrier, len(others))
+
+    made = []
+
+    def copy(slot, to, src=None):
+        at = len(made)
+        made.append(
+            pltpu.make_async_remote_copy(
+                src_ref=whole_ref.at[slot] if src is None else src,
+                dst_ref=whole_ref.at[slot],
+                send_sem=send.at[at], recv_sem=recv.at[at],
+                device_id=(to,), device_id_type=MESH,
+            )
+        )
+        made[-1].start()
+        return made[-1]
+
+    between = [copy(me, device(plane_at(step), chip), shard_ref) for step in range(1, planes)]
+    within, final = [], []
+    for step in range(planes + 1):
+        if step < planes:
+            held = plane_at(-step)
+            slot = device(held, chip)
+            if step > 0:
+                between[step - 1].wait_recv()
+            src = shard_ref if step == 0 else None
+            within.append([copy(slot, device(plane, peer), src) for peer in peers])
+            final.append(copy(slot, partner, src))
+            if step == 0:
+                whole_ref[me] = shard_ref[...]
+        if step > 0:
+            held = plane_at(1 - step)
+            for at, source in enumerate(sources):
+                within[step - 1][at].wait_recv()
+                slot = device(held, source)
+                if relayed and at == 0:
+                    relay = copy(slot, device(plane, peers[1]))
+                final.append(copy(slot, partner))
+            if relayed:
+                relay.wait_recv()
+                final.append(copy(device(held, 3 - chip), partner))
+    for one in final:
+        one.wait_recv()
+    for one in made:
+        one.wait_send()
+
+
+def gather(shard, count, group):
+    planes, chips = count // group, group // 2
+    copies = planes - 1 + planes * (2 * chips - 1)
+    vmem = pl.BlockSpec(memory_space=pltpu.VMEM)
+    return pl.pallas_call(
+        functools.partial(gather_kernel, count, group),
+        out_shape=jax.ShapeDtypeStruct((count,) + shard.shape, shard.dtype),
+        in_specs=[vmem],
+        out_specs=vmem,
+        scratch_shapes=[pltpu.SemaphoreType.DMA((copies,)), pltpu.SemaphoreType.DMA((copies,))],
+        compiler_params=pltpu.CompilerParams(
+            collective_id=1, has_side_effects=True, vmem_limit_bytes=40 * 1024 * 1024
+        ),
+    )(shard)
+
+
 def per_device(image_features, text_features, projections, labels):
     rows, width_in = image_features.shape
     count = lax.axis_size("dp")
     shifts = min(REACH, count // 2)
-    whole = lax.all_gather(projections, "dp", axis=0, tiled=True)
+    whole = gather(projections, count, shifts // 2).reshape(2 * width_in, -1)
     image_weight = whole[:width_in]
     text_weight = whole[width_in:]
     image_unit, image_norm = normalize(

time: 148 us -> 106 us (0.72)
  waiting for transfers between devices: 72 us -> 0 us
  Pallas kernels: 48.2 us -> 92.2 us
  between operations: 14.1 us -> 0.77 us
  matrix products: 10.6 us -> 6.88 us
  local copies, waits for them, and re-layouts: 0.02 us -> 2.43 us
    all_gather x1 -> x0, waiting for transfers between devices: 71.3 us -> none  [per_device(): whole = lax.all_gather(projections, 'dp', axis=0, tiled=True)]
    pallas_call x0 -> x1, Pallas kernels: none -> 36.7 us  [gather(): pl.pallas_call(functools.partial(gather_kernel, count, group), out_shape=...]
    pallas_call x1, Pallas kernels: 48.2 us -> 55.5 us  [pair_grads(): pl.pallas_call(functools.partial(pair_kernel, count, shifts), out_shape=[...]
    unnamed x8 -> x16, local copies, waits for them, and re-layouts: 0.02 us -> 2.03 us
    dot_general x1, matrix products: 2.56 us -> 0.69 us  [per_device(): jnp.dot(image_features, image_weight, preferred_element_type=jnp.float32)]
    dot_general x1, matrix products: 2.43 us -> 0.68 us  [per_device(): jnp.dot(text_features, text_weight, preferred_element_type=jnp.float32)]
  transfers between devices with their start and end apart: 1 -> 0, of which waited for: 1 -> 0; matrix products, arithmetic and copies ran while one was open for 0% -> 0% of each run, Pallas kernels for 0% -> 0%
where the time goes in v2:
time: 106 us; the launch traced here: 105 us
  Pallas kernels  92.2 us (87%)
  matrix products  6.88 us (6%)
  other arithmetic  3.17 us (3%)
  local copies, waits for them, and re-layouts  2.43 us (2%)
    pallas_call x1, Pallas kernels, pair_grads(): pl.pallas_call(functools.partial(pair_kernel, count, shifts), out_shape=[...  55.5 us
    pallas_call x1, Pallas kernels, gather(): pl.pallas_call(functools.partial(gather_kernel, count, group), out_shape=...  36.7 us
    dot_general x1, matrix products, per_device(): lax.dot_general(image_draw, image_weight, contract_last, preferred_elemen...  3.75 us

profile of v2, /device:TPU:0, one launch (start us, length us, event | category | flops | bytes accessed | tf_op | source)
XLA Modules:
  0.0 105.5 jit_solution(1415518526666828867)
XLA Ops:
  0.6 0.0 copy-start
  0.6 0.0 copy-start.1
  0.7 1.0 copy-done.1
  1.6 36.7 %shard_map.59 = bf16[32,72,1152]{2,1,0:T(8,128)(2,1)S(1)} custom-call(bf16[72,1152]{1,0:T(8,128)(2,1)S(1)} %copy-done.1), custom_call_target="tpu_custom_call" | custom-call | tf_op jit(solution)/shard_map/pallas_call | solution.py:289
  38.3 0.4 fusion.8
  38.7 0.0 copy-start.2
  38.8 0.0 copy-start.4
  38.8 0.0 copy-done
  38.8 0.7 multiply_reduce_fusion.3
  39.5 0.0 copy-start.5
  39.5 0.5 copy-done.5
  40.0 0.8 fusion.6.image_ref
  40.8 0.0 copy-done.4
  40.8 0.7 multiply_reduce_fusion.2
  41.5 0.0 copy-done.2
  41.6 0.0 copy-start.6
  41.6 0.5 copy-done.6
  42.1 0.8 fusion.7.text_ref
  42.9 55.5 %shard_map.60 = (f32[128,1152]{1,0:T(8,128)}, f32[128,1152]{1,0:T(8,128)}) custom-call(bf16[128,1152]{1,0:T(8,128)(2,1)} %fusion.6.image_ref, bf16[128,1152]{1,0:T(8,128)(2,1)} %fusion.7.text_ref, s32[1,128]{1,0:T(1,128)} %bitcast.13), custom_call_target="tpu_custom_call" | custom-call | tf_op jit(solution)/shard_map/pallas_call | solution.py:186
  98.4 1.5 %multiply_reduce_fusion = (f32[128]{0:T(128)S(1)}, f32[128]{0:T(128)S(1)}) fusion(f32[128,1152]{1,0:T(8,128)} %get-tuple-element.5, f32[128,1152]{1,0:T(8,128)S(1)} %get-tuple-element.11, f32[128]{0:T(128)} %copy-done.6, f32[128,1152]{1,0:T(8,128)} %get-tuple-element.4, f32[128,1152]{1,0:T(8,128)S(1)} %get-tuple-element.9, f32[128]{0:T(128)} %copy-done.5), kind=kLoop, calls=%fused_computation.1 | loop fusion | flops 884480 | bytes 2361344 | tf_op jit(solution)/shard_map/reduce_sum | solution.py:26
  99.9 0.0 copy-start.3
  99.9 0.0 copy-start.7
  99.9 3.7 %fusion = f32[128,1152]{1,0:T(8,128)} fusion(bf16[1152,1152]{1,0:T(8,128)(2,1)} %bitcast.12, f32[128,1152]{1,0:T(8,128)} %get-tuple-element.4, f32[128]{0:T(128)S(1)} %get-tuple-element.13, f32[128]{0:T(128)} %copy-done.5, f32[128,1152]{1,0:T(8,128)S(1)} %get-tuple-element.9), kind=kOutput, calls=%fused_computation.6 | convolution fusion | flops 340475904 | bytes 4424704 | tf_op jit(solution)/shard_map/dot_general | solution.py:319
  103.7 0.0 copy-done.3
  103.7 0.0 copy-done.7
  103.7 1.8 %fusion.1 = f32[128,1152]{1,0:T(8,128)} fusion(bf16[1152,1152]{1,0:T(8,128)(2,1)S(1)} %bitcast.10, f32[128,1152]{1,0:T(8,128)S(1)} %copy-done.3, f32[128]{0:T(128)S(1)} %get-tuple-element.12, f32[128]{0:T(128)S(1)} %copy-done.7, f32[128,1152]{1,0:T(8,128)S(1)} %get-tuple-element.11), kind=kOutput, calls=%fused_computation.7 | convolution fusion | flops 340475904 | bytes 4424704 | tf_op jit(solution)/shard_map/dot_general | solution.py:322
  (2 shorter events, 0.0 us)
Async XLA Ops:
  0.6 38.1 %copy-start = (bf16[128,1152]{1,0:T(8,128)(2,1)S(1)}, bf16[128,1152]{1,0:T(8,128)(2,1)}, u32[]{:S(2)}) copy-start(bf16[128,1152]{1,0:T(8,128)(2,1)} %param.4) | copy-start | bytes 884740
  0.6 1.0 copy-start.1
  38.7 2.8 %copy-start.2 = (bf16[16,72,1152]{2,1,0:T(8,128)(2,1)}, bf16[16,72,1152]{2,1,0:T(8,128)(2,1)S(1)}, u32[]{:S(2)}) copy-start(bf16[16,72,1152]{2,1,0:T(8,128)(2,1)S(1)} %get-tuple-element.7) | copy-start | bytes 7962628
  38.8 2.1 %copy-start.4 = (bf16[128,1152]{1,0:T(8,128)(2,1)S(1)}, bf16[128,1152]{1,0:T(8,128)(2,1)}, u32[]{:S(2)}) copy-start(bf16[128,1152]{1,0:T(8,128)(2,1)} %param.5) | copy-start | bytes 884740
  39.5 0.5 copy-start.5
  41.6 0.5 copy-start.6
  99.9 3.8 %copy-start.3 = (f32[128,1152]{1,0:T(8,128)S(1)}, f32[128,1152]{1,0:T(8,128)}, u32[]{:S(2)}) copy-start(f32[128,1152]{1,0:T(8,128)} %get-tuple-element.5) | copy-start | bytes 1769476
  99.9 3.8 %copy-start.7 = (f32[128]{0:T(128)S(1)}, f32[128]{0:T(128)}, u32[]{:S(2)}) copy-start(f32[128]{0:T(128)} %copy-done.6) | copy-start | bytes 1540

commit v3 on v2

v3 whole, which is shorter than its diff:
```python
import functools

import jax
import jax.numpy as jnp
from jax import lax
from jax.experimental import pallas as pl
from jax.experimental.pallas import tpu as pltpu
from jax.sharding import PartitionSpec as P

REACH = 32


logit_scale = 10.0
logit_bias = -2.0
eps = 1e-06
contract_last = (((1,), (1,)), ((), ()))
MESH = pl.DeviceIdType.MESH


def normalize(raw):
    norm = jnp.sqrt(jnp.sum(raw * raw, axis=-1, keepdims=True) + eps)
    return (raw / norm, norm)


def unproject(unit, norm, grad):
    inner = jnp.sum(unit * grad, axis=-1, keepdims=True)
    return ((grad - unit * inner) / norm).astype(jnp.bfloat16)


def pair_kernel(
    count, shifts,
    image_ref, texts, label_ref, image_acc, text_acc,
    images, names, coeff, coeff_t, text_sum, over, over_in, total, total_in, back, back_in,
    send, recv,
):
    rows, width = image_ref.shape
    group = shifts // 2
    chips = group // 2
    planes = count // group
    me = lax.axis_index("dp")
    plane, inside = me // group, me % group
    chip, core = inside // 2, inside % 2
    partner = me + 1 - 2 * core

    def chip_at(step):
        return plane * group + lax.rem(chip + step + chips, chips) * 2 + core

    def plane_at(step):
        return lax.rem(plane + step + planes, planes) * group + inside

    barrier = pltpu.get_barrier_semaphore()
    others = [chip_at(step) for step in range(1, chips)]
    others += [plane_at(step) for step in (1, 2, -1, -2)] + [partner]
    for other in others:
        pl.semaphore_signal(barrier, inc=1, device_id=(other,), device_id_type=MESH)
    pl.semaphore_wait(barrier, len(others))

    made = []

    def copy(src, dst, to):
        at = len(made)
        made.append(
            pltpu.make_async_remote_copy(
                src_ref=src, dst_ref=dst, send_sem=send.at[at], recv_sem=recv.at[at],
                device_id=(to,), device_id_type=MESH,
            )
        )
        made[-1].start()
        return made[-1]

    near, far = pl.ds(0, rows), pl.ds(rows, rows)
    across = [
        [
            copy(label_ref, names.at[0, 1], partner),
            copy(image_ref, images.at[0, far], partner),
        ]
    ]
    arrivals = [[]]
    for step in range(1, chips):
        to = chip_at(step)
        arrivals.append(
            [
                copy(label_ref, names.at[step, 0], to),
                copy(image_ref, images.at[step, near], to),
            ]
        )
    images[0, near] = image_ref[...]
    names[0, 0] = label_ref[...]
    lane = lax.broadcasted_iota(jnp.int32, (rows, 1), 0)

    def pass_on(step):
        for one in arrivals[step]:
            one.wait_recv()
        across.append(
            [
                copy(names.at[step, 0], names.at[step, 1], partner),
                copy(images.at[step, near], images.at[step, far], partner),
            ]
        )

    def fill(step):
        source = lax.rem(chip - step + chips, chips)
        logits = logit_scale * lax.dot_general(
            texts[...], images[step], contract_last, preferred_element_type=jnp.float32
        ) + logit_bias
        for age in range(3):
            text_block = lax.rem(me - age * group + count, count)
            ids = text_block * rows + lane
            lines = slice(age * rows, (age + 1) * rows)
            for side in range(2):
                block = plane * group + source * 2 + (core if side == 0 else 1 - core)
                shift = lax.rem(block - text_block + count, count)
                span = slice(side * rows, (side + 1) * rows)
                piece = jax.nn.sigmoid(logits[lines, span])
                piece = piece - (names[step, side] == ids).astype(jnp.float32)
                piece = piece * (shift < shifts).astype(jnp.float32)
                coeff[lines, span] = piece.astype(jnp.bfloat16)
                coeff_t[span, lines] = piece.T.astype(jnp.bfloat16)

    def image_part(side):
        return logit_scale * jnp.dot(
            coeff_t[side * rows : (side + 1) * rows], texts[...],
            preferred_element_type=jnp.float32,
        )

    def text_part(step, age):
        lines = slice(age * rows, (age + 1) * rows)
        part = jnp.dot(coeff[lines], images[step], preferred_element_type=jnp.float32)
        return part if step == 0 else text_sum[lines] + part

    over_copies, total_copies, back_copies = [], [], {}

    def settle(step):
        over_copies[step].wait_recv()
        if step == 0:
            image_acc[...] = image_acc[...] + over_in[0].astype(jnp.float32)
        else:
            total[step] = (kept[step] + over_in[step].astype(jnp.float32)).astype(jnp.bfloat16)
            total_copies.append(copy(total.at[step], total_in.at[step], chip_at(-step)))

    kept = {}
    for step in range(chips):
        for one in across[step]:
            one.wait_recv()
        fill(step)
        if step + 1 < chips:
            pass_on(step + 1)
            for age in range(3):
                text_sum[age * rows : (age + 1) * rows] = text_part(step, age)
        else:
            for age in (2, 1):
                back[age - 1] = (logit_scale * text_part(step, age)).astype(jnp.bfloat16)
                back_copies[age] = copy(back.at[age - 1], back_in.at[age - 1], plane_at(-age))
        over[step] = image_part(1).astype(jnp.bfloat16)
        over_copies.append(copy(over.at[step], over_in.at[step], partner))
        if step == 0:
            image_acc[...] = image_part(0)
        else:
            kept[step] = image_part(0)
        if step > 0:
            settle(step - 1)
        if step + 1 == chips:
            text_acc[...] = logit_scale * text_part(step, 0)
            settle(step)
    for at in range(chips - 1):
        total_copies[at].wait_recv()
        image_acc[...] += total_in[at + 1].astype(jnp.float32)
    for age in (1, 2):
        back_copies[age].wait_recv()
        text_acc[...] += back_in[age - 1].astype(jnp.float32)
    for one in made:
        one.wait_send()


def pair_grads(image_emb, text_embs, labels, count, shifts):
    rows, width = image_emb.shape
    chips = shifts // 4
    low = jnp.bfloat16
    copies = 6 * chips + 2
    vmem = pl.BlockSpec(memory_space=pltpu.VMEM)
    return pl.pallas_call(
        functools.partial(pair_kernel, count, shifts),
        out_shape=[jax.ShapeDtypeStruct((rows, width), jnp.float32)] * 2,
        in_specs=[vmem] * 3,
        out_specs=[vmem] * 2,
        scratch_shapes=[
            pltpu.VMEM((chips, 2 * rows, width), low),
            pltpu.VMEM((chips, 2, 1, rows), jnp.int32),
            pltpu.VMEM((3 * rows, 2 * rows), low),
            pltpu.VMEM((2 * rows, 3 * rows), low),
            pltpu.VMEM((3 * rows, width), jnp.float32),
            pltpu.VMEM((chips, rows, width), low),
            pltpu.VMEM((chips, rows, width), low),
            pltpu.VMEM((chips, rows, width), low),
            pltpu.VMEM((chips, rows, width), low),
            pltpu.VMEM((2, rows, width), low),
            pltpu.VMEM((2, rows, width), low),
            pltpu.SemaphoreType.DMA((copies,)),
            pltpu.SemaphoreType.DMA((copies,)),
        ],
        compiler_params=pltpu.CompilerParams(
            collective_id=0, has_side_effects=True, vmem_limit_bytes=48 * 1024 * 1024
        ),
    )(image_emb, text_embs, labels.reshape(1, rows))


def gather_kernel(count, group, shard_ref, text_ref, whole_ref, texts_ref, send, recv):
    chips, planes = group // 2, count // group
    me = lax.axis_index("dp")
    plane, inside = me // group, me % group
    chip, core = inside // 2, inside % 2
    partner = me + 1 - 2 * core
    relayed = chips == 4
    if relayed:
        low, high = chip + 1 - 2 * lax.rem(chip, 2), lax.rem(chip + 2, 4)
        peers = [low + (high - low) * core, high + (low - high) * core]
        sources = peers
    else:
        peers = [lax.rem(chip + step, chips) for step in range(1, chips)]
        sources = [lax.rem(chip + chips - step, chips) for step in range(1, chips)]

    def plane_at(step):
        return lax.rem(plane + step + planes, planes)

    def device(plane, chip):
        return plane * group + chip * 2 + core

    barrier = pltpu.get_barrier_semaphore()
    others = [device(plane, peer) for peer in peers]
    others += [device(plane_at(step), chip) for step in range(1, planes)] + [partner]
    for other in others:
        pl.semaphore_signal(barrier, inc=1, device_id=(other,), device_id_type=MESH)
    pl.semaphore_wait(barrier, len(others))

    made = []

    def copy(slot, to, src=None, dst=None):
        at = len(made)
        made.append(
            pltpu.make_async_remote_copy(
                src_ref=whole_ref.at[slot] if src is None else src,
                dst_ref=whole_ref.at[slot] if dst is None else dst,
                send_sem=send.at[at], recv_sem=recv.at[at],
                device_id=(to,), device_id_type=MESH,
            )
        )
        made[-1].start()
        return made[-1]

    between = [copy(me, device(plane_at(step), chip), shard_ref) for step in range(1, planes)]
    within, final = [], []
    for step in range(planes + 1):
        if step < planes:
            held = plane_at(-step)
            slot = device(held, chip)
            if step > 0:
                between[step - 1].wait_recv()
            src = shard_ref if step == 0 else None
            within.append([copy(slot, device(plane, peer), src) for peer in peers])
            final.append(copy(slot, partner, src))
            if step == 0:
                whole_ref[me] = shard_ref[...]
                texts_ref[0] = text_ref[...]
            if step == planes - 1:
                for age in (2, 1):
                    to = device(plane_at(age), chip)
                    final.append(copy(None, to, text_ref, texts_ref.at[age]))
        if step > 0:
            held = plane_at(1 - step)
            for at, source in enumerate(sources):
                within[step - 1][at].wait_recv()
                slot = device(held, source)
                if relayed and at == 0:
                    relay = copy(slot, device(plane, peers[1]))
                final.append(copy(slot, partner))
            if relayed:
                relay.wait_recv()
                final.append(copy(device(held, 3 - chip), partner))
    for one in final:
        one.wait_recv()
    for one in made:
        one.wait_send()


def gather(shard, text, count, group):
    planes, chips = count // group, group // 2
    copies = planes + 1 + planes * (2 * chips - 1)
    vmem = pl.BlockSpec(memory_space=pltpu.VMEM)
    return pl.pallas_call(
        functools.partial(gather_kernel, count, group),
        out_shape=[
            jax.ShapeDtypeStruct((count,) + shard.shape, shard.dtype),
            jax.ShapeDtypeStruct((3,) + text.shape, text.dtype),
        ],
        in_specs=[vmem] * 2,
        out_specs=[vmem] * 2,
        scratch_shapes=[pltpu.SemaphoreType.DMA((copies,)), pltpu.SemaphoreType.DMA((copies,))],
        compiler_params=pltpu.CompilerParams(
            collective_id=1, has_side_effects=True, vmem_limit_bytes=40 * 1024 * 1024
        ),
    )(shard, text)


def per_device(image_features, text_features, projections, labels):
    rows, width_in = image_features.shape
    count = lax.axis_size("dp")
    shifts = min(REACH, count // 2)
    whole, texts = gather(projections, text_features, count, shifts // 2)
    whole = whole.reshape(2 * width_in, -1)
    image_weight = whole[:width_in]
    text_weight = whole[width_in:]
    image_unit, image_norm = normalize(
        jnp.dot(image_features, image_weight, preferred_element_type=jnp.float32)
    )
    text_units, text_norms = normalize(
        jnp.dot(
            texts.reshape(3 * rows, width_in), text_weight, preferred_element_type=jnp.float32
        )
    )
    text_unit, text_norm = text_units[:rows], text_norms[:rows]
    image_acc, text_acc = pair_grads(
        image_unit.astype(jnp.bfloat16), text_units.astype(jnp.bfloat16), labels, count, shifts
    )
    image_draw = unproject(image_unit, image_norm, image_acc)
    text_draw = unproject(text_unit, text_norm, text_acc)
    image_grad = lax.dot_general(
        image_draw, image_weight, contract_last, preferred_element_type=jnp.float32
    )
    text_grad = lax.dot_general(
        text_draw, text_weight, contract_last, preferred_element_type=jnp.float32
    )
    return (image_grad, text_grad)


def solution(mesh):
    placed = (P("dp", None), P("dp", None), P("dp", None), P("dp"))
    return jax.shard_map(
        per_device,
        mesh=mesh,
        in_specs=placed,
        out_specs=(P("dp", None), P("dp", None)),
        check_vma=False,
    )
```

time: 106 us -> 99 us (0.934)
  the two profiles are of different devices: /device:TPU:0 before, /device:TPU:9 now
where the time goes in v3:
time: 99 us; the launch traced here: 98.8 us
  Pallas kernels  84.7 us (86%)
  matrix products  7.73 us (8%)
  local copies, waits for them, and re-layouts  5 us (5%)
    pallas_call x1, Pallas kernels, pair_grads(): pl.pallas_call(functools.partial(pair_kernel, count, shifts), out_shape=[...  48 us
    pallas_call x1, Pallas kernels, gather(): pl.pallas_call(functools.partial(gather_kernel, count, group), out_shape=...  36.6 us
    dot_general x1, matrix products, per_device(): jnp.dot(texts.reshape(3 * rows, width_in), text_weight, preferred_element...  3.28 us
    unnamed x14, local copies, waits for them, and re-layouts  2.85 us

profile of v3, /device:TPU:9, one launch (start us, length us, event | category | flops | bytes accessed | tf_op | source)
XLA Modules:
  0.0 98.8 jit_solution(159467089213310020)
XLA Ops:
  0.6 0.0 copy-start
  0.6 0.0 copy-start.1
  0.7 1.0 %copy-done.1 = bf16[128,1152]{1,0:T(8,128)(2,1)S(1)} copy-done((bf16[128,1152]{1,0:T(8,128)(2,1)S(1)}, bf16[128,1152]{1,0:T(8,128)(2,1)}, u32[]{:S(2)}) %copy-start.1) | copy-done | bytes 294936
  1.7 0.0 copy-start.2
  1.7 0.9 copy-done.2
  2.6 36.6 %shard_map.59 = (bf16[32,72,1152]{2,1,0:T(8,128)(2,1)S(1)}, bf16[3,128,1152]{2,1,0:T(8,128)(2,1)S(1)}) custom-call(bf16[72,1152]{1,0:T(8,128)(2,1)S(1)} %copy-done.2, bf16[128,1152]{1,0:T(8,128)(2,1)S(1)} %copy-done.1), custom_call_target="tpu_custom_call" | custom-call | tf_op jit(solution)/shard_map/pallas_call | solution.py:289
  39.2 1.9 %fusion.12 = (bf16[16,72,1152]{2,1,0:T(8,128)(2,1)}, bf16[16,72,1152]{2,1,0:T(8,128)(2,1)S(1)}) fusion(bf16[32,72,1152]{2,1,0:T(8,128)(2,1)S(1)} %get-tuple-element.6), kind=kLoop, calls=%fused_computation.22 | loop fusion | bytes 10616832 | tf_op jit(solution)/shard_map/slice | solution.py:311
  41.1 0.0 copy-start.4
  41.1 0.0 copy-done
  41.1 0.9 multiply_reduce_fusion.2
  42.1 0.6 copy-done.4
  42.7 0.2 copy.6
  42.9 0.1 bitcast_convert_fusion.image_ref
  43.0 3.3 %multiply_reduce_fusion = (f32[384]{0:T(512)S(1)}, f32[384,1152]{1,0:T(8,128)S(1)}) fusion(bf16[384,1152]{1,0:T(8,128)(2,1)S(1)} %bitcast.24, bf16[1152,1152]{1,0:T(8,128)(2,1)} %bitcast.27), kind=kOutput, calls=%fused_computation | convolution fusion | flops 1020100224 | bytes 5309952 | tf_op jit(solution)/shard_map/dot_general | solution.py:316
  46.3 0.0 copy-start.3
  46.3 0.3 fusion.11
  46.6 0.0 copy-start.6
  46.6 0.3 copy-done.3
  47.0 48.0 %shard_map.60 = (f32[128,1152]{1,0:T(8,128)S(1)}, f32[128,1152]{1,0:T(8,128)S(1)}) custom-call(bf16[128,1152]{1,0:T(8,128)(2,1)S(1)} %bitcast_convert_fusion.image_ref, bf16[384,1152]{1,0:T(8,128)(2,1)S(1)} %get-tuple-element.10.texts, s32[1,128]{1,0:T(1,128)S(1)} %bitcast.23), custom_call_target="tpu_custom_call" | custom-call | tf_op jit(solution)/shard_map/pallas_call | solution.py:181
  95.0 0.3 fusion
  95.3 0.0 copy-start.5
  95.3 0.0 copy-done.6
  95.3 1.8 %fusion.4 = f32[128,1152]{1,0:T(8,128)} fusion(bf16[1152,1152]{1,0:T(8,128)(2,1)S(1)} %bitcast.28, f32[128,1152]{1,0:T(8,128)S(1)} %get-tuple-element.9, f32[384,1152]{1,0:T(8,128)S(1)} %get-tuple-element.11, f32[128]{0:T(128)S(1)} %slice.24, f32[128]{0:T(128)S(1)} %get-tuple-element.19), kind=kOutput, calls=%fused_computation.12 | convolution fusion | flops 340328448 | bytes 4424704 | tf_op jit(solution)/shard_map/dot_general | solution.py:329
  97.1 0.0 copy-done.5
  97.1 1.8 %fusion.5 = f32[128,1152]{1,0:T(8,128)} fusion(bf16[1152,1152]{1,0:T(8,128)(2,1)S(1)} %bitcast.26, f32[128,1152]{1,0:T(8,128)S(1)} %get-tuple-element.8, f32[128]{0:T(128)S(1)} %add_sqrt_fusion.1, f32[128]{0:T(128)S(1)} %get-tuple-element.18, f32[1152,128]{0,1:T(8,128)S(1)} %copy.6), kind=kOutput, calls=%fused_computation.13 | convolution fusion | flops 340475904 | bytes 4424704 | tf_op jit(solution)/shard_map/dot_general | solution.py:326
  (3 shorter events, 0.0 us)
Async XLA Ops:
  0.6 40.5 %copy-start = (bf16[128,1152]{1,0:T(8,128)(2,1)S(1)}, bf16[128,1152]{1,0:T(8,128)(2,1)}, u32[]{:S(2)}) copy-start(bf16[128,1152]{1,0:T(8,128)(2,1)} %param.4) | copy-start | bytes 884740
  0.6 1.0 %copy-start.1 = (bf16[128,1152]{1,0:T(8,128)(2,1)S(1)}, bf16[128,1152]{1,0:T(8,128)(2,1)}, u32[]{:S(2)}) copy-start(bf16[128,1152]{1,0:T(8,128)(2,1)} %text_ref.1) | copy-start | bytes 884740
  1.7 0.9 copy-start.2
  41.1 1.5 %copy-start.4 = (bf16[16,72,1152]{2,1,0:T(8,128)(2,1)}, bf16[16,72,1152]{2,1,0:T(8,128)(2,1)S(1)}, u32[]{:S(2)}) copy-start(bf16[16,72,1152]{2,1,0:T(8,128)(2,1)S(1)} %get-tuple-element.13) | copy-start | bytes 7962628
  46.3 0.7 copy-start.3
  46.6 48.7 %copy-start.6 = (bf16[16,72,1152]{2,1,0:T(8,128)(2,1)S(1)}, bf16[16,72,1152]{2,1,0:T(8,128)(2,1)}, u32[]{:S(2)}) copy-start(bf16[16,72,1152]{2,1,0:T(8,128)(2,1)} %get-tuple-element.12) | copy-start | bytes 7962628
  95.3 1.8 %copy-start.5 = (bf16[16,72,1152]{2,1,0:T(8,128)(2,1)S(1)}, bf16[16,72,1152]{2,1,0:T(8,128)(2,1)}, u32[]{:S(2)}) copy-start(bf16[16,72,1152]{2,1,0:T(8,128)(2,1)} %copy-done.4) | copy-start | bytes 7962628

commit v4 on v3

--- a/solution.py
+++ b/solution.py
@@ -249,6 +249,8 @@
 
     between = [copy(me, device(plane_at(step), chip), shard_ref) for step in range(1, planes)]
     within, final = [], []
+    for age in (2, 1):
+        final.append(copy(None, device(plane_at(age), chip), text_ref, texts_ref.at[age]))
     for step in range(planes + 1):
         if step < planes:
             held = plane_at(-step)
@@ -261,10 +263,6 @@
             if step == 0:
                 whole_ref[me] = shard_ref[...]
                 texts_ref[0] = text_ref[...]
-            if step == planes - 1:
-                for age in (2, 1):
-                    to = device(plane_at(age), chip)
-                    final.append(copy(None, to, text_ref, texts_ref.at[age]))
         if step > 0:
             held = plane_at(1 - step)
             for at, source in enumerate(sources):

time: 99 us -> 102 us (1.030)
  the two profiles are of different devices: /device:TPU:9 before, /device:TPU:8 now
where the time goes in v4:
time: 102 us
  Pallas kernels  88.1 us (86%)
  matrix products  7.73 us (8%)
  local copies, waits for them, and re-layouts  5 us (5%)
    pallas_call x1, Pallas kernels, pair_grads(): pl.pallas_call(functools.partial(pair_kernel, count, shifts), out_shape=[...  44.1 us
    pallas_call x1, Pallas kernels, gather(): pl.pallas_call(functools.partial(gather_kernel, count, group), out_shape=...  44 us
    dot_general x1, matrix products, per_device(): jnp.dot(texts.reshape(3 * rows, width_in), text_weight, preferred_element...  3.27 us
    unnamed x14, local copies, waits for them, and re-layouts  2.85 us

profile of v4, /device:TPU:8, one launch (start us, length us, event | category | flops | bytes accessed | tf_op | source)
XLA Modules:
  0.0 102.2 jit_solution(13196175140542999217)
XLA Ops:
  0.6 0.0 copy-start
  0.6 0.0 copy-start.1
  0.7 1.0 copy-done.1
  1.7 0.0 copy-start.2
  1.7 0.9 copy-done.2
  2.6 44.0 %shard_map.59 = (bf16[32,72,1152]{2,1,0:T(8,128)(2,1)S(1)}, bf16[3,128,1152]{2,1,0:T(8,128)(2,1)S(1)}) custom-call(bf16[72,1152]{1,0:T(8,128)(2,1)S(1)} %copy-done.2, bf16[128,1152]{1,0:T(8,128)(2,1)S(1)} %copy-done.1), custom_call_target="tpu_custom_call" | custom-call | tf_op jit(solution)/shard_map/pallas_call | solution.py:287
  46.6 1.9 %fusion.12 = (bf16[16,72,1152]{2,1,0:T(8,128)(2,1)}, bf16[16,72,1152]{2,1,0:T(8,128)(2,1)S(1)}) fusion(bf16[32,72,1152]{2,1,0:T(8,128)(2,1)S(1)} %get-tuple-element.6), kind=kLoop, calls=%fused_computation.22 | loop fusion | bytes 10616832 | tf_op jit(solution)/shard_map/slice | solution.py:309
  48.5 0.0 copy-start.4
  48.5 0.0 copy-done
  48.5 0.9 multiply_reduce_fusion.2
  49.4 0.6 copy-done.4
  50.0 0.2 copy.6
  50.2 0.1 bitcast_convert_fusion.image_ref
  50.4 3.3 %multiply_reduce_fusion = (f32[384]{0:T(512)S(1)}, f32[384,1152]{1,0:T(8,128)S(1)}) fusion(bf16[384,1152]{1,0:T(8,128)(2,1)S(1)} %bitcast.24, bf16[1152,1152]{1,0:T(8,128)(2,1)} %bitcast.27), kind=kOutput, calls=%fused_computation | convolution fusion | flops 1020100224 | bytes 5309952 | tf_op jit(solution)/shard_map/dot_general | solution.py:314
  53.6 0.0 copy-start.3
  53.7 0.3 fusion.11
  54.0 0.0 copy-start.6
  54.0 0.3 copy-done.3
  54.3 44.1 %shard_map.60 = (f32[128,1152]{1,0:T(8,128)S(1)}, f32[128,1152]{1,0:T(8,128)S(1)}) custom-call(bf16[128,1152]{1,0:T(8,128)(2,1)S(1)} %bitcast_convert_fusion.image_ref, bf16[384,1152]{1,0:T(8,128)(2,1)S(1)} %get-tuple-element.10.texts, s32[1,128]{1,0:T(1,128)S(1)} %bitcast.23), custom_call_target="tpu_custom_call" | custom-call | tf_op jit(solution)/shard_map/pallas_call | solution.py:181
  98.4 0.3 fusion
  98.7 0.0 copy-start.5
  98.7 0.0 copy-done.6
  98.7 1.8 %fusion.4 = f32[128,1152]{1,0:T(8,128)} fusion(bf16[1152,1152]{1,0:T(8,128)(2,1)S(1)} %bitcast.28, f32[128,1152]{1,0:T(8,128)S(1)} %get-tuple-element.9, f32[384,1152]{1,0:T(8,128)S(1)} %get-tuple-element.11, f32[128]{0:T(128)S(1)} %slice.24, f32[128]{0:T(128)S(1)} %get-tuple-element.19), kind=kOutput, calls=%fused_computation.12 | convolution fusion | flops 340328448 | bytes 4424704 | tf_op jit(solution)/shard_map/dot_general | solution.py:327
  100.5 0.0 copy-done.5
  100.5 1.8 %fusion.5 = f32[128,1152]{1,0:T(8,128)} fusion(bf16[1152,1152]{1,0:T(8,128)(2,1)S(1)} %bitcast.26, f32[128,1152]{1,0:T(8,128)S(1)} %get-tuple-element.8, f32[128]{0:T(128)S(1)} %add_sqrt_fusion.1, f32[128]{0:T(128)S(1)} %get-tuple-element.18, f32[1152,128]{0,1:T(8,128)S(1)} %copy.6), kind=kOutput, calls=%fused_computation.13 | convolution fusion | flops 340475904 | bytes 4424704 | tf_op jit(solution)/shard_map/dot_general | solution.py:324
  (3 shorter events, 0.0 us)
Async XLA Ops:
  0.6 47.8 %copy-start = (bf16[128,1152]{1,0:T(8,128)(2,1)S(1)}, bf16[128,1152]{1,0:T(8,128)(2,1)}, u32[]{:S(2)}) copy-start(bf16[128,1152]{1,0:T(8,128)(2,1)} %param.4) | copy-start | bytes 884740
  0.6 1.0 copy-start.1
  1.7 0.9 copy-start.2
  48.5 1.5 %copy-start.4 = (bf16[16,72,1152]{2,1,0:T(8,128)(2,1)}, bf16[16,72,1152]{2,1,0:T(8,128)(2,1)S(1)}, u32[]{:S(2)}) copy-start(bf16[16,72,1152]{2,1,0:T(8,128)(2,1)S(1)} %get-tuple-element.13) | copy-start | bytes 7962628
  53.6 0.7 copy-start.3
  54.0 44.7 %copy-start.6 = (bf16[16,72,1152]{2,1,0:T(8,128)(2,1)S(1)}, bf16[16,72,1152]{2,1,0:T(8,128)(2,1)}, u32[]{:S(2)}) copy-start(bf16[16,72,1152]{2,1,0:T(8,128)(2,1)} %get-tuple-element.12) | copy-start | bytes 7962628
  98.7 1.8 %copy-start.5 = (bf16[16,72,1152]{2,1,0:T(8,128)(2,1)S(1)}, bf16[16,72,1152]{2,1,0:T(8,128)(2,1)}, u32[]{:S(2)}) copy-start(bf16[16,72,1152]{2,1,0:T(8,128)(2,1)} %copy-done.4) | copy-start | bytes 7962628
